TPU v7x, 32 devices: a whole 2x2x4 slice. The times are simulated.
32 devices in a mesh: shard: 2 (over core), model: 4 (over y, x), unit: 4 (over z).
Axes of the slice: x: 2, y: 2, z: 4, core: 2. Of those that a mesh axis runs over, the one named last changes fastest.
Arguments:
- train_query: bfloat16 [16384, 4096], P(('unit', 'shard'), 'model'), parts along dimension 0, may hold values from -0.125 to 0.125
- low_query: bfloat16 [16384, 16], P(('unit', 'shard')), parts along dimension 0, may hold values from -0.09375 to 0.09375
- high_query: bfloat16 [64, 4096], P('unit', 'model'), parts along dimension 0, may hold values from -1.5 to 1.5
- train_key: bfloat16 [16384, 1024], P(('unit', 'shard'), 'model'), parts along dimension 0, may hold values from -0.125 to 0.125
- low_key: bfloat16 [16384, 16], P(('unit', 'shard')), parts along dimension 0, may hold values from -0.09375 to 0.09375
- high_key: bfloat16 [64, 1024], P('unit', 'model'), parts along dimension 0, may hold values from -1.5 to 1.5
- train_value: bfloat16 [16384, 1024], P(('unit', 'shard'), 'model'), parts along dimension 0, may hold values from -0.125 to 0.125
- low_value: bfloat16 [16384, 16], P(('unit', 'shard')), parts along dimension 0, may hold values from -0.09375 to 0.09375
- high_value: bfloat16 [64, 1024], P('unit', 'model'), parts along dimension 0, may hold values from -1.5 to 1.5
- norm_train: float32 [16384], P(('unit', 'shard', 'model')), parts along dimension 0, may hold values from 0.25 to 1.75
- norm_step: float32 [16384], P(('unit', 'shard', 'model')), parts along dimension 0, may hold values from -0.3 to 0.3
Outputs:
- serving_query: bfloat16 [16384, 4096], P('unit', 'model'), parts along dimension 0
- serving_key: bfloat16 [16384, 1024], P('unit', 'model'), parts along dimension 0
- serving_value: bfloat16 [16384, 1024], P('unit', 'model'), parts along dimension 0
- scale_query: float32 [16384], P(('unit', 'model')), parts along dimension 0
- scale_key: float32 [4096], P(('unit', 'model')), parts along dimension 0
- scale_value: float32 [4096], P(('unit', 'model')), parts along dimension 0
- serve_norm: bfloat16 [16384], P('unit'), parts along dimension 0
There are 4 independent parts, one for each index of `unit`. A program takes and returns all parts, laid end to end along the dimension named above; each array names one. Nothing has to cross between parts.
All inputs are finite; a program needn't handle non-finite values. Where the computation divides by a largest or mean magnitude, that divisor is 1e-20 or more.
Results may differ from a plain program's by a relative error of at most 0.001.
Values may be sent and summed in bfloat16 or wider, within the bound.
A program may use at most 64 MiB of HBM per device.

v0:
```python
import functools

import jax
import jax.numpy as jnp
from jax import lax
from jax.experimental import pallas as pl
from jax.experimental.pallas import tpu as pltpu
from jax.sharding import PartitionSpec as P

mix_rate = 1.0
MESH = pl.DeviceIdType.MESH
MIB = 1 << 20


def exchange_kernel(
    n_shard,
    n_model,
    tile,
    tq, lq, hq, tk, lk, hk, tv, lv, hv, nt, ns,
    wq, wk, wv, sq, sk, sv, norm,
    base_q, base_k, base_v, low_q, low_k, low_v, high_q, high_k, high_v, norms,
    send_base, recv_base, send_low, recv_low, local_high, send_norm, recv_norm,
):
    trains, lows, highs = (tq, tk, tv), (lq, lk, lv), (hq, hk, hv)
    bases, low_bufs, high_bufs = (base_q, base_k, base_v), (low_q, low_k, low_v), (high_q, high_k, high_v)
    wholes, scales = (wq, wk, wv), (sq, sk, sv)
    rows = tq.shape[0]
    steps = rows // tile
    shard, model = lax.axis_index("shard"), lax.axis_index("model")
    group = n_shard * n_model
    place = shard * n_model + model

    barrier = pltpu.get_barrier_semaphore()
    for k in range(1, group):
        other = lax.rem(place + k, group)
        pl.semaphore_signal(
            barrier, inc=1,
            device_id={"shard": other // n_model, "model": lax.rem(other, n_model)},
            device_id_type=MESH,
        )

    def own_base(t, i):
        at = pl.ds(t * tile, tile)
        return pltpu.make_async_copy(trains[i].at[at, :], bases[i].at[0, at, :], recv_base.at[0, t, i])

    local = []
    for i in range(3):
        local.append(pltpu.make_async_copy(lows[i], low_bufs[i].at[0], recv_low.at[0, i]))
        local.append(pltpu.make_async_copy(highs[i], high_bufs[i], local_high.at[i]))
    for copy in local:
        copy.start()
    for t in range(steps):
        for i in range(3):
            own_base(t, i).start()
    own_norm = [
        pltpu.make_async_copy(source, norms.at[place, j], recv_norm.at[0, j])
        for j, source in enumerate((nt, ns))
    ]
    for copy in own_norm:
        copy.start()
    pl.semaphore_wait(barrier, group - 1)

    def low_copy(d, i):
        return pltpu.make_async_remote_copy(
            src_ref=lows[i], dst_ref=low_bufs[i].at[d],
            send_sem=send_low.at[d, i], recv_sem=recv_low.at[d, i],
            device_id={"shard": lax.rem(shard + d, n_shard)}, device_id_type=MESH,
        )

    def base_copy(d, t, i):
        at = pl.ds(t * tile, tile)
        return pltpu.make_async_remote_copy(
            src_ref=trains[i].at[at, :], dst_ref=bases[i].at[d, at, :],
            send_sem=send_base.at[d, t, i], recv_sem=recv_base.at[d, t, i],
            device_id={"shard": lax.rem(shard + d, n_shard)}, device_id_type=MESH,
        )

    def norm_copy(k, j):
        other = lax.rem(place + k, group)
        return pltpu.make_async_remote_copy(
            src_ref=(nt, ns)[j], dst_ref=norms.at[place, j],
            send_sem=send_norm.at[k, j], recv_sem=recv_norm.at[k, j],
            device_id={"shard": other // n_model, "model": lax.rem(other, n_model)},
            device_id_type=MESH,
        )

    for d in range(1, n_shard):
        for i in range(3):
            low_copy(d, i).start()
    for t in range(steps):
        for d in range(1, n_shard):
            for i in range(3):
                base_copy(d, t, i).start()
    for k in range(1, group):
        for j in range(2):
            norm_copy(k, j).start()

    def merge(d, t, tops):
        first = lax.rem(shard - d + n_shard, n_shard) * rows
        at = pl.multiple_of(t * tile, tile)
        to = pl.multiple_of(first + at, tile)
        new = []
        for i in range(3):
            top = tops[i]
            product = lax.dot_general(
                low_bufs[i][d, :, pl.ds(at, tile)], high_bufs[i][...],
                (((0,), (0,)), ((), ())), preferred_element_type=jnp.float32,
            )
            whole = bases[i][d, pl.ds(at, tile), :].astype(jnp.float32) + mix_rate * product
            wholes[i][pl.ds(to, tile), :] = whole
            top = jnp.maximum(top, jnp.max(jnp.abs(whole).reshape(tile // 8, 8, whole.shape[1]), axis=0))
            new.append(top)
        return tuple(new)

    tops = tuple(jnp.zeros((8, h.shape[1]), jnp.float32) for h in high_bufs)
    for copy in local:
        copy.wait()

    def own_step(t, tops):
        for i in range(3):
            own_base(t, i).wait()
        return merge(0, t, tops)

    tops = lax.fori_loop(0, steps, own_step, tops)
    for d in range(1, n_shard):
        for i in range(3):
            low_copy(d, i).wait()

    def other_step(u, tops):
        t, d = u // (n_shard - 1), 1 + lax.rem(u, n_shard - 1)
        for i in range(3):
            base_copy(d, t, i).wait()
        return merge(d, t, tops)

    tops = lax.fori_loop(0, steps * (n_shard - 1), other_step, tops)
    for i in range(3):
        scales[i][...] = jnp.max(tops[i], axis=0, keepdims=True)
    for copy in own_norm:
        copy.wait()
    for k in range(1, group):
        for j in range(2):
            norm_copy(k, j).wait()
    norm[...] = (norms[:, 0] + norms[:, 1]).reshape(norm.shape).astype(norm.dtype)


def scale_kernel(
    plan,
    wq, wk, wv, sq, sk, sv, norm,
    oq, ok, ov, osq, osk, osv, onorm,
    buf_q, buf_k, buf_v, sems, small_sems,
):
    wholes, scales = (wq, wk, wv), (sq, sk, sv)
    outs, bufs = (oq, ok, ov), (buf_q, buf_k, buf_v)
    small = [
        pltpu.make_async_copy(source, target, small_sems.at[n])
        for n, (source, target) in enumerate(((sq, osq), (sk, osk), (sv, osv), (norm, onorm)))
    ]
    for copy in small:
        copy.start()
    for i, step, count, base in plan:
        inverse = 1.0 / scales[i][...]

        def copy(t):
            at = pl.multiple_of(t * step, step)
            return pltpu.make_async_copy(
                bufs[i].at[pl.ds(at, step), :], outs[i].at[pl.ds(at, step), :], sems.at[base + t]
            )

        @pl.loop(0, count)
        def _(t):
            at = pl.multiple_of(t * step, step)
            bufs[i][pl.ds(at, step), :] = (wholes[i][pl.ds(at, step), :] * inverse).astype(bufs[i].dtype)
            copy(t).start()

    for i, step, count, base in plan:
        @pl.loop(0, count)
        def _(t):
            at = pl.multiple_of(t * step, step)
            pltpu.make_async_copy(
                bufs[i].at[pl.ds(at, step), :], outs[i].at[pl.ds(at, step), :], sems.at[base + t]
            ).wait()
    for copy in small:
        copy.wait()


def local(n_shard, n_model, tq, lq, hq, tk, lk, hk, tv, lv, hv, nt, ns):
    rows, rank = tq.shape[0], hq.shape[0]
    widths = (tq.shape[1], tk.shape[1], tv.shape[1])
    tile = min(rows, 256)
    steps = rows // tile
    group = n_shard * n_model
    lanes = 128 if nt.shape[0] % 128 == 0 else nt.shape[0]
    piece = (nt.shape[0] // lanes, lanes)
    full = n_shard * rows
    f32, bf16 = jnp.float32, jnp.bfloat16
    dma = pltpu.SemaphoreType.DMA
    hbm, vmem = pl.BlockSpec(memory_space=pltpu.HBM), pl.BlockSpec(memory_space=pltpu.VMEM)
    norm_shape = (group * piece[0], lanes)

    parts = pl.pallas_call(
        functools.partial(exchange_kernel, n_shard, n_model, tile),
        out_shape=[pltpu.VMEM((full, w), f32) for w in widths]
        + [pltpu.VMEM((1, w), f32) for w in widths]
        + [pltpu.VMEM(norm_shape, bf16)],
        in_specs=[hbm] * 11,
        out_specs=[vmem] * 7,
        scratch_shapes=[pltpu.VMEM((n_shard, rows, w), bf16) for w in widths]
        + [pltpu.VMEM((n_shard, rank, rows), bf16)] * 3
        + [pltpu.VMEM((rank, w), bf16) for w in widths]
        + [
            pltpu.VMEM((group, 2) + piece, f32),
            dma((n_shard, steps, 3)), dma((n_shard, steps, 3)),
            dma((n_shard, 3)), dma((n_shard, 3)), dma((3,)),
            dma((group, 2)), dma((group, 2)),
        ],
        compiler_params=pltpu.CompilerParams(
            collective_id=0, has_side_effects=True, vmem_limit_bytes=18 * MIB
        ),
        cost_estimate=pl.CostEstimate(flops=0, bytes_accessed=40 * MIB, transcendentals=0),
        name="exchange",
    )(*(pltpu.with_memory_space_constraint(x, pltpu.HBM) for x in (tq, lq.T, hq, tk, lk.T, hk, tv, lv.T, hv, nt.reshape(piece), ns.reshape(piece))))

    plan, base = [], 0
    for i in (0, 1, 2):
        step = min(full, 256 * max(widths) // widths[i])
        plan.append((i, step, full // step, base))
        base += full // step
    outs = pl.pallas_call(
        functools.partial(scale_kernel, tuple(plan)),
        out_shape=[jax.ShapeDtypeStruct((full, w), bf16) for w in widths]
        + [jax.ShapeDtypeStruct((1, w), f32) for w in widths]
        + [jax.ShapeDtypeStruct(norm_shape, bf16)],
        in_specs=[pl.BlockSpec(memory_space=pltpu.VMEM)] * 7,
        out_specs=[hbm] * 7,
        scratch_shapes=[pltpu.VMEM((full, w), bf16) for w in widths] + [dma((base,)), dma((4,))],
        compiler_params=pltpu.CompilerParams(vmem_limit_bytes=18 * MIB),
        cost_estimate=pl.CostEstimate(flops=0, bytes_accessed=40 * MIB, transcendentals=0),
        name="scale",
    )(*(pltpu.with_memory_space_constraint(x, pltpu.VMEM) for x in parts))
    return (*outs[:3], *(o.reshape(-1) for o in outs[3:]))


def solution(mesh):
    in_specs = (
        P(("unit", "shard"), "model"),
        P(("unit", "shard"), None),
        P("unit", "model"),
        P(("unit", "shard"), "model"),
        P(("unit", "shard"), None),
        P("unit", "model"),
        P(("unit", "shard"), "model"),
        P(("unit", "shard"), None),
        P("unit", "model"),
        P(("unit", "shard", "model")),
        P(("unit", "shard", "model")),
    )
    out_specs = (
        P("unit", "model"),
        P("unit", "model"),
        P("unit", "model"),
        P(("unit", "model")),
        P(("unit", "model")),
        P(("unit", "model")),
        P("unit"),
    )
    body = functools.partial(local, mesh.shape["shard"], mesh.shape["model"])
    return jax.shard_map(body, mesh=mesh, in_specs=in_specs, out_specs=out_specs, check_vma=False)
```

profile of v0, /device:TPU:0, one launch (start us, length us, event | category | flops | bytes accessed | tf_op | source)
XLA Modules:
  0.0 21.6 jit_solution(1657321071858887787)
XLA Ops:
  0.6 16.1 %exchange.1 = (f32[4096,1024]{1,0:T(8,128)S(1)}, f32[4096,256]{1,0:T(8,128)S(1)}, f32[4096,256]{1,0:T(8,128)S(1)}, f32[1,1024]{1,0:T(1,128)S(1)}, f32[1,256]{1,0...) custom-call(bf16[2048,1024]{1,0:T(8,128)(2,1)} %tq.1, bf16[16,2048]{1,0:T(8,128)(2,1)} %bitcast.9, ...), custom_call_target="tpu_custom_call" | custom-call | bytes 41943040 | tf_op jit(solution)/shard_map/exchange/pallas_call | solution.py:200
  16.7 4.9 %scale.1 = (bf16[4096,1024]{1,0:T(8,128)(2,1)}, bf16[4096,256]{1,0:T(8,128)(2,1)}, bf16[4096,256]{1,0:T(8,128)(2,1)}, f32[1,1024]{1,0:T(1,128)}, f32[1,256]{1,0:...) custom-call(f32[4096,1024]{1,0:T(8,128)S(1)} %get-tuple-element.21.wq, f32[4096,256]{1,0:T(8,128)S(1)} %get-tuple-element.22.wk, ...), custom_call_target="tpu_custom_call" | custom-call | bytes 41943040 | tf_op jit(solution)/shard_map/scale/pallas_call | solution.py:228
where the time goes:
time: 21.7 us; the launch traced here: 21.6 us
  Pallas kernels  20.9 us (96%)
  between operations  0.64 us (3%)
    pallas_call x1, Pallas kernels, local(): pl.pallas_call(functools.partial(exchange_kernel, n_shard, n_model, tile)...  16.1 us
    pallas_call x1, Pallas kernels, local(): pl.pallas_call(functools.partial(scale_kernel, tuple(plan)), out_shape=[j...  4.86 us

commit v1 on v0

v1 whole, which is shorter than its diff:
```python
import functools

import jax
import jax.numpy as jnp
from jax import lax
from jax.experimental import pallas as pl
from jax.experimental.pallas import tpu as pltpu
from jax.sharding import PartitionSpec as P


mix_rate = 1.0
MIB = 1 << 20
f32, bf16 = jnp.float32, jnp.bfloat16
HBM, VMEM = pl.BlockSpec(memory_space=pltpu.HBM), pl.BlockSpec(memory_space=pltpu.VMEM)
DMA = pltpu.SemaphoreType.DMA
MESH = pl.DeviceIdType.MESH


def in_hbm(x):
    return pltpu.with_memory_space_constraint(x, pltpu.HBM)


def in_vmem(x):
    return pltpu.with_memory_space_constraint(x, pltpu.VMEM)


def product(low, rank, i, at, tile, high):
    return mix_rate * lax.dot_general(
        low[pl.ds(i * rank, rank), pl.ds(at, tile)], high[...],
        (((0,), (0,)), ((), ())), preferred_element_type=f32,
    )


def merge_kernel(n_shard, n_model, tile, first, rank, offsets, *refs):
    refs = list(refs)
    take = lambda n: [refs.pop(0) for _ in range(n)]
    trains, lows, highs = zip(*(take(3) for _ in range(3)))
    nt, ns = take(2)
    raws = take(1) if first < trains[0].shape[0] else []
    bufs, scales = take(3), take(3)
    norm, gq, far_low = take(3)
    wholes = take(3)
    low, gk, gv, raw_q, raw_k, raw_v = take(6)
    fars, products = take(3), take(3)
    norms, packs, sem_base, sem_small = take(4)
    send_norm, recv_norm, send_low, recv_low, send_far, recv_far, send_pack, recv_pack, ready, all_in = take(10)
    highs_in = (gq, gk, gv)
    rows = trains[0].shape[0]
    steps = rows // tile
    shard, model = lax.axis_index("shard"), lax.axis_index("model")
    group = n_shard * n_model
    place = shard * n_model + model
    lead = n_shard - 1
    leads, follows = shard == lead, shard != lead
    others = range(1, n_shard)

    def far(k):
        other = lax.rem(place + k, group)
        return {"shard": other // n_model, "model": lax.rem(other, n_model)}

    def near(d):
        return {"shard": lax.rem(shard + d, n_shard)}

    def remote(source, target, send, recv, device):
        return pltpu.make_async_remote_copy(
            src_ref=source, dst_ref=target, send_sem=send, recv_sem=recv,
            device_id=device, device_id_type=MESH,
        )

    def signal(semaphore, device):
        pl.semaphore_signal(semaphore, inc=1, device_id=device, device_id_type=MESH)

    barrier = pltpu.get_barrier_semaphore()
    for d in others:
        @pl.when(lax.rem(shard + d, n_shard) != lead)
        def _():
            signal(barrier, near(d))

    small = []
    for i in range(3):
        small.append(pltpu.make_async_copy(lows[i], low.at[pl.ds(i * rank, rank), :], sem_small.at[2 * i]))
        small.append(pltpu.make_async_copy(highs[i], highs_in[i], sem_small.at[2 * i + 1]))
    own_norm = [pltpu.make_async_copy(x, norms.at[place, j], sem_small.at[6 + j]) for j, x in enumerate((nt, ns))]
    for copy in own_norm + small:
        copy.start(priority=0)
    parts = [(0, first, raw_q)] + [(first, rows - first, raw) for raw in raws]

    def own_at(i, begin, count):
        if i:
            return (raw_k, raw_v)[i - 1].at[pl.ds(begin, count), :]
        start, _, ref = [p for p in parts if p[0] <= begin < p[0] + p[1]][0]
        return ref.at[pl.ds(begin - start, count), :]

    copies = [
        [
            pltpu.make_async_copy(trains[i].at[pl.ds(t * tile, tile), :], own_at(i, t * tile, tile), sem_base.at[t, i])
            for i in range(3)
        ]
        for t in range(steps)
    ]
    for t in range(steps):
        for copy in copies[t]:
            copy.start(priority=1)

    @pl.when(leads)
    def _():
        pl.semaphore_wait(ready, n_shard - 1)
        for m in range(1, n_model):
            signal(barrier, {"model": lax.rem(model + m, n_model)})

    @pl.when(follows)
    def _():
        pl.semaphore_wait(barrier, n_shard - 1)
        signal(ready, {"shard": lead})

    low_copies = [
        remote(lows[i], far_low.at[d - 1, pl.ds(i * rank, rank), :], send_low.at[d, i], recv_low.at[d, i], near(d))
        for d in others for i in range(3)
    ]
    far_copies = {}

    def pieces(i, count, size):
        for t in range(count // size):
            at = pl.ds(t * size, size)
            far_copies[i, t] = [
                remote(
                    trains[i].at[at, :], fars[i].at[d - 1, at, :],
                    send_far.at[i, t, d], recv_far.at[i, t, d], near(d),
                )
                for d in others
            ]

    sizes = (min(tile, first), rows // 2, rows // 4)
    counts = (first // sizes[0], 2, 4)
    for i in range(3):
        pieces(i, first if i == 0 else rows, sizes[i])

    def start(groups):
        for group_copies in groups:
            for copy in group_copies:
                copy.start()

    norm_copies = [
        remote(norms.at[place], norms.at[place], send_norm.at[k], recv_norm.at[k], far(k)) for k in range(1, group)
    ]

    def meet():
        @pl.when(leads)
        def _():
            pl.semaphore_wait(barrier, n_model - 1)
            for d in others:
                signal(all_in, near(d))

        @pl.when(follows)
        def _():
            pl.semaphore_wait(all_in, 1)

        start([norm_copies])

    keys, values = ([far_copies[i, t] for t in range(counts[i])] for i in (1, 2))
    early, late = model == 0, model == n_model - 1
    between = jnp.logical_not(jnp.logical_or(early, late))

    @pl.when(early)
    def _():
        start([low_copies] + keys + values + [far_copies[0, 0]])

    @pl.when(between)
    def _():
        start([low_copies] + keys + values[:1])

    for copy in own_norm:
        copy.wait()

    @pl.when(late)
    def _():
        meet()
        start([low_copies] + keys + values + [far_copies[0, 0]])

    for copy in small:
        copy.wait()
    for i in (1, 2):
        wholes[i][...] = product(low, rank, i, 0, rows, highs_in[i])
    wholes[0][...] = product(low, rank, 0, 0, rows, highs_in[0])

    @pl.when(between)
    def _():
        meet()
        start(values[1:] + [far_copies[0, 0]])

    tops = [jnp.zeros((8, h.shape[1]), f32) for h in highs]
    for t in range(steps):
        for copy in copies[t]:
            copy.wait()
        here = pl.ds(t * tile, tile)
        for i in range(3):
            whole = own_at(i, t * tile, tile)[...].astype(f32) + wholes[i][here, :]
            wholes[i][here, :] = whole
            tops[i] = jnp.maximum(tops[i], jnp.max(jnp.abs(whole).reshape(tile // 8, 8, whole.shape[1]), axis=0))
    packs[0] = jnp.zeros(packs.shape[1:], f32)
    for i in range(3):
        top = jnp.max(tops[i], axis=0, keepdims=True)
        for j in range(top.shape[1] // 128):
            packs[0, pl.ds(offsets[i] + j, 1), :] = top[:, j * 128:(j + 1) * 128]
    pack_copies = [remote(packs.at[0], packs.at[d], send_pack.at[d], recv_pack.at[d], near(d)) for d in others]
    start([pack_copies] + [far_copies[0, t] for t in range(1, counts[0])])
    for copy in low_copies:
        copy.wait()
    limits = (first, rows, rows)
    for d in range(n_shard - 1):
        for i in (1, 2, 0):
            products[i][d] = product(far_low.at[d], rank, i, 0, limits[i], highs_in[i])

    @pl.when(early)
    def _():
        meet()

    for copy in pack_copies:
        copy.wait()
    top = packs[0]
    for d in others:
        top = jnp.maximum(top, packs[d])
    inverse = []
    for i in range(3):
        block = top[offsets[i]:offsets[i] + scales[i].shape[1] // 128, :]
        line = jnp.concatenate([block[j:j + 1, :] for j in range(block.shape[0])], axis=1)
        scales[i][...] = line
        inverse.append(1.0 / line)
    for t in range(steps):
        at = pl.ds(t * tile, tile)
        for i in range(3):
            bufs[i][at, :] = (wholes[i][at, :] * inverse[i]).astype(bf16)
    for i in (1, 2, 0):
        for t in range(counts[i]):
            for copy in far_copies[i, t]:
                copy.wait()
            at = pl.ds(t * sizes[i], sizes[i])
            for d in range(n_shard - 1):
                whole = fars[i][d, at, :].astype(f32) + products[i][d, at, :]
                to = pl.ds(rows + d * limits[i] + t * sizes[i], sizes[i])
                bufs[i][to, :] = (whole * inverse[i]).astype(bf16)
    for copy in norm_copies:
        copy.wait()
    norm[...] = (norms[:, 0] + norms[:, 1]).reshape(norm.shape).astype(norm.dtype)


def write_kernel(rank, n_shard, first, rows, *refs):
    refs = list(refs)
    take = lambda n: [refs.pop(0) for _ in range(n)]
    bufs, scales = take(3), take(3)
    norm, gq, far_low = take(3)
    outs, lines = take(3), take(3)
    (norm_out,) = take(1)
    rest = take(1) if first < rows else []
    sems, small = take(2)
    shard = lax.axis_index("shard")
    made = []
    for i in (0, 1, 2):
        count = rows if i else first
        half = rows // 2
        for h in range(2):
            base = pl.multiple_of(shard * rows + h * half, half)
            made.append(pltpu.make_async_copy(
                bufs[i].at[pl.ds(h * half, half), :], outs[i].at[pl.ds(base, half), :], sems.at[i, 0, h]
            ))
        for d in range(1, n_shard):
            base = pl.multiple_of(lax.rem(shard + n_shard - d, n_shard) * rows, rows)
            made.append(pltpu.make_async_copy(
                bufs[i].at[pl.ds(rows + (d - 1) * count, count), :], outs[i].at[pl.ds(base, count), :], sems.at[i, d, 0]
            ))
    for i in range(3):
        made.append(pltpu.make_async_copy(scales[i], lines[i], small.at[i]))
    made.append(pltpu.make_async_copy(norm, norm_out, small.at[3]))
    for copy in made:
        copy.start()
    for r in rest:
        for d in range(n_shard - 1):
            r[d] = product(far_low.at[d], rank, 0, first, rows - first, gq)
    for copy in made:
        copy.wait()


def chunk_kernel(tile, n_shard, begin, rows, *refs):
    refs = list(refs)
    take = lambda n: [refs.pop(0) for _ in range(n)]
    _, scale, rest = take(3)
    raws = take(n_shard - 1)
    out, buf, sems = take(3)
    count = raws[0].shape[0]
    shard = lax.axis_index("shard")
    inverse = 1.0 / scale[...]
    made = []
    for d in range(1, n_shard):
        base = lax.rem(shard + n_shard - d, n_shard) * rows
        for t in range(count // tile):
            at = pl.ds(t * tile, tile)
            here = pl.ds((d - 1) * count + t * tile, tile)
            whole = raws[d - 1][at, :].astype(f32) + rest[d - 1, at, :]
            buf[here, :] = (whole * inverse).astype(bf16)
            there = pl.multiple_of(base + begin + t * tile, tile)
            made.append(pltpu.make_async_copy(buf.at[here, :], out.at[pl.ds(there, tile), :], sems.at[d, t]))
            made[-1].start()
    for copy in made:
        copy.wait()


def shift(x, axis, size, d):
    return lax.ppermute(x, axis, [(s, (s + d) % size) for s in range(size)])


def split(rows):
    tile = min(rows, 256)
    units = rows // tile
    return tile, tile * max(1, units // 2)


def local(n_shard, n_model, tq, lq, hq, tk, lk, hk, tv, lv, hv, nt, ns):
    rows, rank = tq.shape[0], hq.shape[0]
    widths = (tq.shape[1], tk.shape[1], tv.shape[1])
    tile, first = split(rows)
    steps = rows // tile
    group = n_shard * n_model
    full = n_shard * rows
    left = rows - first
    lanes = 128 if nt.shape[0] % 128 == 0 else nt.shape[0]
    piece = (nt.shape[0] // lanes, lanes)
    offsets, at = [], 0
    for w in widths:
        offsets.append(at)
        at += w // 128
    pack_rows = -(-at // 8) * 8
    others = range(1, n_shard)
    far = n_shard - 1
    limits = (first, rows, rows)
    cost = lambda size: pl.CostEstimate(flops=size, bytes_accessed=size, transcendentals=0)
    vm = pltpu.VMEM
    norm_shape = (group * piece[0], lanes)
    elements = sum(widths)
    scratch_bytes = 4 * rows * elements + 2 * rows * elements + 2 * full * elements + 4 * full * elements

    merged = pl.pallas_call(
        functools.partial(merge_kernel, n_shard, n_model, tile, first, rank, tuple(offsets)),
        out_shape=([vm((left, widths[0]), bf16)] if left else [])
        + [vm((rows + far * n, w), bf16) for n, w in zip(limits, widths)]
        + [vm((1, w), f32) for w in widths]
        + [vm(norm_shape, bf16), vm((rank, widths[0]), bf16), vm((far, 3 * rank, rows), bf16)],
        in_specs=[HBM] * 11,
        out_specs=[VMEM] * (9 + bool(left)),
        scratch_shapes=[vm((rows, w), f32) for w in widths]
        + [
            vm((3 * rank, rows), bf16), vm((rank, widths[1]), bf16), vm((rank, widths[2]), bf16),
            vm((first, widths[0]), bf16), vm((rows, widths[1]), bf16), vm((rows, widths[2]), bf16),
        ]
        + [vm((far, n, w), bf16) for n, w in zip(limits, widths)]
        + [vm((far, n, w), f32) for n, w in zip(limits, widths)]
        + [
            vm((group, 2) + piece, f32), vm((n_shard, pack_rows, 128), f32), DMA((steps, 3)), DMA((8,)),
            DMA((group,)), DMA((group,)), DMA((n_shard, 3)), DMA((n_shard, 3)),
            DMA((3, max(steps, 4), n_shard)), DMA((3, max(steps, 4), n_shard)), DMA((n_shard,)), DMA((n_shard,)),
            pltpu.SemaphoreType.REGULAR, pltpu.SemaphoreType.REGULAR,
        ],
        compiler_params=pltpu.CompilerParams(
            collective_id=0, has_side_effects=True, vmem_limit_bytes=min(40 * MIB, scratch_bytes + 4 * MIB),
        ),
        cost_estimate=cost(10**9),
        name="merge",
    )(*(in_hbm(x) for x in (tq, lq.T, hq, tk, lk.T, hk, tv, lv.T, hv, nt.reshape(piece), ns.reshape(piece))))
    query = [in_vmem(shift(merged[0], "shard", n_shard, d)) for d in others] if left else []
    merged = [in_vmem(x) for x in merged[bool(left):]]

    outs = pl.pallas_call(
        functools.partial(write_kernel, rank, n_shard, first, rows),
        out_shape=[jax.ShapeDtypeStruct((full, w), bf16) for w in widths]
        + [jax.ShapeDtypeStruct((1, w), f32) for w in widths]
        + [jax.ShapeDtypeStruct(norm_shape, bf16)]
        + ([vm((far, left, widths[0]), f32)] if left else []),
        in_specs=[VMEM] * 9,
        out_specs=[HBM] * 7 + [VMEM] * bool(left),
        scratch_shapes=[DMA((3, n_shard, 2)), DMA((4,))],
        compiler_params=pltpu.CompilerParams(vmem_limit_bytes=2 * MIB),
        cost_estimate=cost(10**9),
        name="write",
    )(*merged)
    oq, ok, ov, sq, sk, sv, norm = outs[:7]

    if left:
        step = min(tile, left)
        oq = pl.pallas_call(
            functools.partial(chunk_kernel, step, n_shard, first, rows),
            out_shape=jax.ShapeDtypeStruct((full, widths[0]), bf16),
            in_specs=[HBM] + [VMEM] * (2 + far),
            out_specs=HBM,
            scratch_shapes=[vm((far * left, widths[0]), bf16), DMA((n_shard, left // step))],
            input_output_aliases={0: 0},
            compiler_params=pltpu.CompilerParams(vmem_limit_bytes=2 * MIB + 2 * far * left * widths[0]),
            cost_estimate=cost(10**8),
            name="chunk",
        )(oq, merged[3], in_vmem(outs[7]), *query)
    return (oq, ok, ov, *(x.reshape(-1) for x in (sq, sk, sv, norm)))


def solution(mesh):
    in_specs = (
        P(("unit", "shard"), "model"),
        P(("unit", "shard"), None),
        P("unit", "model"),
        P(("unit", "shard"), "model"),
        P(("unit", "shard"), None),
        P("unit", "model"),
        P(("unit", "shard"), "model"),
        P(("unit", "shard"), None),
        P("unit", "model"),
        P(("unit", "shard", "model")),
        P(("unit", "shard", "model")),
    )
    out_specs = (
        P("unit", "model"),
        P("unit", "model"),
        P("unit", "model"),
        P(("unit", "model")),
        P(("unit", "model")),
        P(("unit", "model")),
        P("unit"),
    )
    n_shard, n_model = mesh.shape["shard"], mesh.shape["model"]

    def body(*args):
        return local(n_shard, n_model, *args)

    return jax.shard_map(body, mesh=mesh, in_specs=in_specs, out_specs=out_specs, check_vma=False)
```

time: 21.7 us -> 16.9 us (0.78)
  the two profiles are of different devices: /device:TPU:0 before, /device:TPU:7 now
where the time goes in v1:
time: 16.9 us; the launch traced here: 16.8 us
  Pallas kernels  15.9 us (94%)
  between operations  0.66 us (4%)
  starting transfers between devices  0.2 us (1%)
    pallas_call x1, Pallas kernels, local(): pl.pallas_call(functools.partial(merge_kernel, n_shard, n_model, tile, fi...  10.3 us
    pallas_call x1, Pallas kernels, local(): pl.pallas_call(functools.partial(write_kernel, rank, n_shard, first, rows...  4.09 us
    pallas_call x1, Pallas kernels, local(): pl.pallas_call(functools.partial(chunk_kernel, step, n_shard, first, rows...  1.51 us
  transfers between devices with their start and end apart: 1, of which 0 were waited for; matrix products, arithmetic and copies ran while one was open for 0% of the time, Pallas kernels for 24%

profile of v1, /device:TPU:7, one launch (start us, length us, event | category | flops | bytes accessed | tf_op | source)
XLA Modules:
  0.0 16.8 jit_solution(11370228356567829400)
XLA Ops:
  0.6 10.3 %merge.1 = (bf16[1024,1024]{1,0:T(8,128)(2,1)S(1)}, bf16[3072,1024]{1,0:T(8,128)(2,1)S(1)}, bf16[4096,256]{1,0:T(8,128)(2,1)S(1)}, bf16[4096,256]{1,0:T(8,128)(2...) custom-call(bf16[2048,1024]{1,0:T(8,128)(2,1)} %refs_0_.1, ...), custom_call_target="tpu_custom_call" | custom-call | flops 1000000000 | bytes 1000000000 | tf_op jit(solution)/shard_map/merge/pallas_call | solution.py:341
  11.0 0.2 %collective-permute-start = (bf16[1024,1024]{1,0:T(8,128)(2,1)S(1)}, bf16[1024,1024]{1,0:T(8,128)(2,1)S(1)}, u32[]{:S(2)}, u32[]{:S(2)}) collective-permute-start(bf16[1024,1024]{1,0:T(8,128)(2,1)S(1)} %get-tuple-element.36), channel_id=1, source_target_pairs={{0,16},{16,0},{1,17},{17,1},{2,18},{18,2},{3,19},{19,3},{4,20},{20... | collective-permute-start | bytes 6291464 | tf_op jit(solution)/shard_map/ppermute | solution.py:308
  11.2 4.1 %write.1 = (bf16[4096,1024]{1,0:T(8,128)(2,1)}, bf16[4096,256]{1,0:T(8,128)(2,1)}, bf16[4096,256]{1,0:T(8,128)(2,1)}, f32[1,1024]{1,0:T(1,128)}, f32[1,256]{1,0:...) custom-call(bf16[3072,1024]{1,0:T(8,128)(2,1)S(1)} %get-tuple-element.25.refs_0_, ...), custom_call_target="tpu_custom_call" | custom-call | flops 1000000000 | bytes 1000000000 | tf_op jit(solution)/shard_map/write/pallas_call | solution.py:371
  15.3 0.0 collective-permute-done.refs_3_
  15.3 1.5 %chunk.1 = bf16[4096,1024]{1,0:T(8,128)(2,1)} custom-call(bf16[4096,1024]{1,0:T(8,128)(2,1)} %get-tuple-element.34.refs_0_, f32[1,1024]{1,0:T(1,128)S(1)} %get-tuple-element.28.refs_3_.refs_1_, f32[1,1024,1024]{2,1,0:T(8,128)S(1)} %get-tuple-element.35.refs_2_, bf16[1024,1024]{1,0:T(8,128)(2,1)S(1)} %collective-permute-done.refs_3_), custom_call_target="tpu_custom_call", output_to_operand_aliasing={{}: (0, {})} | custom-call | flops 100000000 | bytes 100000000 | tf_op jit(solution)/shard_map/chunk/pallas_call | solution.py:388
Async XLA Ops:
  11.0 4.3 %collective-permute-start = (bf16[1024,1024]{1,0:T(8,128)(2,1)S(1)}, bf16[1024,1024]{1,0:T(8,128)(2,1)S(1)}, u32[]{:S(2)}, u32[]{:S(2)}) collective-permute-start(bf16[1024,1024]{1,0:T(8,128)(2,1)S(1)} %get-tuple-element.36), channel_id=1, source_target_pairs={{0,16},{16,0},{1,17},{17,1},{2,18},{18,2},{3,19},{19,3},{4,20},{20... | collective-permute-start | bytes 6291464 | tf_op jit(solution)/shard_map/ppermute | solution.py:308
